TPU v7x, 32 devices: a whole 2x2x4 slice. The times are simulated.
32 devices in a mesh: groups: 2 (over y), cells: 8 (over z, x), side: 2 (over core).
Axes of the slice: x: 2, y: 2, z: 4, core: 2. Of those that a mesh axis runs over, the one named last changes fastest.
Arguments:
- datasets: float32 [2, 2000, 8192], P('side', None, ('groups', 'cells')), parts along dimension 2, may hold values from -6 to 6
- sketch: float32 [64, 8192], P(None, ('groups', 'cells')), parts along dimension 1, may hold values from -6 to 6
Outputs:
- factors: float32 [2, 64, 8192], P('side', None, ('groups', 'cells')), parts along dimension 2
There are 2 independent parts, one for each index of `groups`. A program takes and returns all parts, laid end to end along the dimension named above; each array names one. Nothing has to cross between parts.
All inputs are finite; a program needn't handle non-finite values.
Results may differ from a plain program's by a relative error of at most 0.00009.
Values sent between devices are 32-bit elements; how exact they have to be, the bound alone decides.
A program may use at most 64 MiB of HBM per device.

v0:
```python
import jax
import jax.numpy as jnp
from jax import lax
from jax.sharding import PartitionSpec as P


def from_behind(value, axis, steps):
    count = lax.axis_size(axis)
    initial, last = (max(0, -steps), min(count, count - steps))
    return lax.ppermute(value, axis, [(source, source + steps) for source in range(initial, last)])


def per_device(datasets, sketch):
    high = lax.Precision.HIGHEST
    own_data = datasets[0]
    side_index = lax.axis_index("side")
    cell_count = own_data.shape[1] * lax.axis_size("cells")
    scale = jnp.sqrt(jnp.float32(cell_count))
    partial_value = jnp.dot(sketch, own_data.T, precision=high)
    summed = lax.psum(partial_value, "cells")
    arrived = from_behind(summed, "side", -1)
    panel = jnp.where(side_index == 0, arrived, summed)
    range_rows = jnp.dot(panel, own_data, precision=high)
    gram_part = jnp.dot(range_rows, range_rows.T, precision=high)
    raw_part = jnp.dot(range_rows, own_data.T, precision=high)
    gram, raw_cross = lax.psum((gram_part, raw_part), "cells")
    lower = jnp.linalg.cholesky(gram)
    basis = jax.scipy.linalg.solve_triangular(lower, range_rows, lower=True)
    cross = jax.scipy.linalg.solve_triangular(lower, raw_cross, lower=True)
    received = from_behind(cross, "side", 1)
    projected = jnp.dot(received, own_data, precision=high)
    result = jnp.where(side_index == 0, basis * scale, projected / scale)
    return result[None]


def solution(mesh):
    in_specs = (P("side", None, ("groups", "cells")), P(None, ("groups", "cells")))
    out_specs = P("side", None, ("groups", "cells"))
    return jax.shard_map(
        per_device, mesh=mesh, in_specs=in_specs, out_specs=out_specs, check_vma=False
    )
```

profile of v0, /device:TPU:0, one launch (start us, length us, event | category | flops | bytes accessed | tf_op | source)
XLA Modules:
  0.0 225.7 jit_solution(7290744189002880673)
XLA Ops:
  6.5 0.0 copy-start
  6.5 0.0 all-reduce.3.cloned.1.call-start
  6.5 0.9 copy-done
  7.4 6.7 %fusion.6 = f32[64,2000]{1,0:T(8,128)} fusion(f32[64,512]{1,0:T(8,128)S(1)} %copy-done, f32[1,2000,512]{2,1,0:T(8,128)} %param.2), kind=kOutput, calls=%fused_computation.6 | convolution fusion | flops 786432000 | bytes 4739072 | tf_op jit(solution)/shard_map/dot_general | solution.py:19
  14.1 0.0 all-reduce.3.cloned.1.call-update
  14.2 0.0 all-reduce.5.cloned.1.call-start
  14.2 75.5 %all-reduce.3.cloned.1.call-done = f32[64,2000]{1,0:T(8,128)} async-done(((f32[64,2000]{1,0:T(8,128)}), f32[64,2000]{1,0:T(8,128)}) %all-reduce.3.cloned.1.call-update) | async-done | bytes 512016 | tf_op jit(solution)/shard_map/psum | solution.py:20
  89.7 1.3 collective-permute-start
  91.0 0.0 copy-start.1
  91.0 2.7 %collective-permute-done = f32[64,2000]{1,0:T(8,128)S(1)} collective-permute-done((f32[64,2000]{1,0:T(8,128)}, f32[64,2000]{1,0:T(8,128)S(1)}, u32[]{:S(2)}, u32[]{:S(2)}) %collective-permute-start) | collective-permute-done | bytes 512032 | tf_op jit(solution)/shard_map/ppermute | solution.py:10
  93.7 4.8 %fusion.4 = f32[64,512]{1,0:T(8,128)S(1)} fusion(f32[1,2000,512]{2,1,0:T(8,128)} %param.2, f32[64,2000]{1,0:T(8,128)S(1)} %collective-permute-done, f32[64,2000]{1,0:T(8,128)} %all-reduce.3.cloned.1.call-done, pred[]{:T(512)S(6)} %eq.4), kind=kOutput, calls=%fused_computation.4 | convolution fusion | flops 786560000 | bytes 5251073 | tf_op jit(solution)/shard_map/dot_general | solution.py:23
  98.5 0.3 fusion.24
  98.7 0.0 copy-done.1
  98.7 4.6 %fusion.2 = f32[64,2000]{1,0:T(8,128)} fusion(f32[64,512]{1,0:T(8,128)S(1)} %fusion.4, f32[1,2000,512]{2,1,0:T(8,128)S(1)} %copy-done.1), kind=kOutput, calls=%fused_computation.2 | convolution fusion | flops 786432000 | bytes 4739072 | tf_op jit(solution)/shard_map/dot_general | solution.py:25
  103.3 35.4 %psum.22 = f32[64,64]{0,1:T(8,128)S(1)} all-reduce(f32[64,64]{0,1:T(8,128)S(1)} %fusion.24), channel_id=1, replica_groups=mesh['groups'=2,'cells'=8,'side'=2] {'cells'}, use_global_device_ids=true, to_apply=%region_1.2 | all-reduce | flops 4096 | bytes 32768 | tf_op jit(solution)/shard_map/psum | solution.py:26
  138.7 0.1 copy.4
  138.8 0.0 all-reduce.5.cloned.1.call-update
  138.8 5.8 %cholesky.16 = f32[64,64]{1,0:T(8,128)S(1)} custom-call(f32[64,64]{1,0:T(8,128)S(1)} %fusion.23), custom_call_target="Cholesky" | custom-call | tf_op jit(solution)/shard_map/jit(cholesky)/cholesky | solution.py:27
  144.7 0.6 compare_reduce_fusion
  145.3 0.7 fusion.19
  146.0 4.9 %custom-call.10 = f32[1,64,64]{1,2,0:T(8,128)S(1)} custom-call(f32[1,64,64]{2,1,0:T(8,128)S(1)} %fusion.19), custom_call_target="InvertDiagBlocksLowerTriangular" | custom-call | tf_op jit(solution)/shard_map/jit(_solve_triangular)/triangular_solve | solution.py:28
  150.9 58.1 %all-reduce.5.cloned.1.call-done = f32[64,2000]{1,0:T(8,128)} async-done(((f32[64,2000]{1,0:T(8,128)}), f32[64,2000]{1,0:T(8,128)}) %all-reduce.5.cloned.1.call-update) | async-done | bytes 512016 | tf_op jit(solution)/shard_map/psum | solution.py:26
  209.0 1.7 fusion.20
  210.6 1.3 collective-permute-start.1
  212.0 0.3 convolution_multiply_fusion
  212.3 1.2 collective-permute-done.1
  213.5 5.4 %fusion.14 = f32[1,64,512]{2,1,0:T(8,128)} fusion(f32[64,512]{1,0:T(8,128)S(1)} %convolution_multiply_fusion, f32[64,2000]{1,0:T(8,128)S(1)} %collective-permute-done.1, f32[1,2000,512]{2,1,0:T(8,128)} %param.2, pred[]{:T(512)S(6)} %eq.4), kind=kOutput, calls=%fused_computation.10 | convolution fusion | flops 786497536 | bytes 4870145 | tf_op jit(solution)/shard_map/dot_general | solution.py:31
  (2 shorter events, 0.0 us)
Async XLA Ops:
  6.5 0.9 copy-start
  6.5 83.2 %all-reduce.3.cloned.1.call-start = ((), (), s32[]{:S(2)}) async-start(), calls=%async_computation | async-start | bytes 1048576 | tf_op jit(solution)/shard_map/psum | solution.py:20
  14.2 194.8 %all-reduce.5.cloned.1.call-start = ((), (), s32[]{:S(2)}) async-start(), calls=%async_computation.1 | async-start | bytes 1048576 | tf_op jit(solution)/shard_map/psum | solution.py:26
  89.7 4.0 %collective-permute-start = (f32[64,2000]{1,0:T(8,128)}, f32[64,2000]{1,0:T(8,128)S(1)}, u32[]{:S(2)}, u32[]{:S(2)}) collective-permute-start(f32[64,2000]{1,0:T(8,128)} %all-reduce.3.cloned.1.call-done), channel_id=1, source_target_pairs={{1,0},{3,2},{5,4},{7,6},{9,8},{11,10},{13,12},{15,14},{17,16},{19,... | collective-permute-start | bytes 1536008 | tf_op jit(solution)/shard_map/ppermute | solution.py:10
  91.0 7.7 %copy-start.1 = (f32[1,2000,512]{2,1,0:T(8,128)S(1)}, f32[1,2000,512]{2,1,0:T(8,128)}, u32[]{:S(2)}) copy-start(f32[1,2000,512]{2,1,0:T(8,128)} %param.2) | copy-start | bytes 12288004
  210.6 2.8 %collective-permute-start.1 = (f32[64,2000]{1,0:T(8,128)S(1)}, f32[64,2000]{1,0:T(8,128)S(1)}, u32[]{:S(2)}, u32[]{:S(2)}) collective-permute-start(f32[64,2000]{1,0:T(8,128)S(1)} %fusion.20), channel_id=1, source_target_pairs={{0,1},{2,3},{4,5},{6,7},{8,9},{10,11},{12,13},{14,15},{16,17},{18,... | collective-permute-start | bytes 1536008 | tf_op jit(solution)/shard_map/ppermute | solution.py:10
Sparse Core Ops, SparseCore 0:
  14.3 75.3 all-reduce.2
  138.9 70.0 all-reduce.4
where the time goes:
time: 226 us
  waiting for transfers between devices  137 us (61%)
  blocking collectives  35.4 us (16%)
  matrix products  23.7 us (10%)
  between operations  13.5 us (6%)
  other arithmetic  12.1 us (5%)
  starting transfers between devices  2.65 us (1%)
    psum x1, waiting for transfers between devices, per_device(): summed = lax.psum(partial_value, 'cells')  75.5 us
    psum x1, waiting for transfers between devices, per_device(): gram, raw_cross = lax.psum((gram_part, raw_part), 'cells')  58.1 us
    psum x1, blocking collectives, per_device(): gram, raw_cross = lax.psum((gram_part, raw_part), 'cells')  35.4 us
    dot_general x1, matrix products, per_device(): partial_value = jnp.dot(sketch, own_data.T, precision=high)  6.69 us
    another operation x3, other arithmetic, per_device(): lower = jnp.linalg.cholesky(gram)  6.52 us
    another operation x2, other arithmetic, per_device(): basis = jax.scipy.linalg.solve_triangular(lower, range_rows, lower=True)  5.55 us
    dot_general x1, matrix products, per_device(): projected = jnp.dot(received, own_data, precision=high)  5.43 us
    dot_general x1, matrix products, per_device(): range_rows = jnp.dot(panel, own_data, precision=high)  4.75 us
  transfers between devices with their start and end apart: 4, of which 4 were waited for; matrix products, arithmetic and copies ran while one was open for 5% of the time, Pallas kernels for 0%

commit v1 on v0

--- a/solution.py
+++ b/solution.py
@@ -17,7 +17,13 @@
     cell_count = own_data.shape[1] * lax.axis_size("cells")
     scale = jnp.sqrt(jnp.float32(cell_count))
     partial_value = jnp.dot(sketch, own_data.T, precision=high)
-    summed = lax.psum(partial_value, "cells")
+    degree = lax.axis_size("cells")
+    summed = partial_value
+    for k in [
+        [(dev_j, dev_j ^ jj) for dev_j in range(degree)] for jj in (1, 2, 4, 8, 16) if jj < degree
+    ]:
+        field_out = lax.ppermute(summed, "cells", k)
+        summed = summed + field_out
     arrived = from_behind(summed, "side", -1)
     panel = jnp.where(side_index == 0, arrived, summed)
     range_rows = jnp.dot(panel, own_data, precision=high)

time: 226 us -> 204 us (0.903)
  waiting for transfers between devices: 137 us -> 107 us
  starting transfers between devices: 2.65 us -> 10.4 us
    psum x1 -> x0, waiting for transfers between devices: 75.5 us -> none  [per_device(): summed = lax.psum(partial_value, 'cells')]
    ppermute x0 -> x3, waiting for transfers between devices: none -> 45 us  [per_device(): field_out = lax.ppermute(summed, 'cells', k)]
    ppermute x0 -> x3, starting transfers between devices: none -> 7.56 us  [per_device(): field_out = lax.ppermute(summed, 'cells', k)]
  transfers between devices with their start and end apart: 4 -> 6, of which waited for: 4 -> 6; matrix products, arithmetic and copies ran while one was open for 5% -> 6% of each run, Pallas kernels for 0% -> 0%
where the time goes in v1:
time: 204 us
  waiting for transfers between devices  107 us (52%)
  blocking collectives  37 us (18%)
  matrix products  22.9 us (11%)
  between operations  13.5 us (7%)
  other arithmetic  12.3 us (6%)
  starting transfers between devices  10.4 us (5%)
    psum x1, waiting for transfers between devices, per_device(): gram, raw_cross = lax.psum((gram_part, raw_part), 'cells')  58.2 us
    ppermute x3, waiting for transfers between devices, per_device(): field_out = lax.ppermute(summed, 'cells', k)  45 us
    psum x1, blocking collectives, per_device(): gram, raw_cross = lax.psum((gram_part, raw_part), 'cells')  37 us
    ppermute x3, starting transfers between devices, per_device(): field_out = lax.ppermute(summed, 'cells', k)  7.56 us
    another operation x3, other arithmetic, per_device(): lower = jnp.linalg.cholesky(gram)  6.52 us
    dot_general x1, matrix products, per_device(): partial_value = jnp.dot(sketch, own_data.T, precision=high)  5.88 us
    another operation x2, other arithmetic, per_device(): basis = jax.scipy.linalg.solve_triangular(lower, range_rows, lower=True)  5.55 us
    dot_general x1, matrix products, per_device(): projected = jnp.dot(received, own_data, precision=high)  5.42 us
  transfers between devices with their start and end apart: 6, of which 6 were waited for; matrix products, arithmetic and copies ran while one was open for 6% of the time, Pallas kernels for 0%

profile of v1, /device:TPU:0, one launch (start us, length us, event | category | flops | bytes accessed | tf_op | source)
XLA Modules:
  0.0 203.7 jit_solution(6312519002897353469)
XLA Ops:
  6.5 0.0 copy-start
  6.5 0.0 all-reduce.2.cloned.1.call-start
  6.5 0.9 copy-done
  7.4 5.9 %fusion.6 = f32[64,2000]{1,0:T(8,128)S(1)} fusion(f32[64,512]{1,0:T(8,128)S(1)} %copy-done, f32[1,2000,512]{2,1,0:T(8,128)} %param.2), kind=kOutput, calls=%fused_computation.6 | convolution fusion | flops 786432000 | bytes 4739072 | tf_op jit(solution)/shard_map/dot_general | solution.py:19
  13.3 3.0 %collective-permute-start = (f32[64,2000]{1,0:T(8,128)S(1)}, f32[64,2000]{1,0:T(8,128)S(1)}, u32[]{:S(2)}, u32[]{:S(2)}) collective-permute-start(f32[64,2000]{1,0:T(8,128)S(1)} %fusion.6), channel_id=1, source_target_pairs={{0,2},{2,0},{4,6},{6,4},{8,10},{10,8},{12,14},{14,12},{1,3},{3,1},... | collective-permute-start | bytes 1536008 | tf_op jit(solution)/shard_map/ppermute | solution.py:25
  16.4 11.9 %collective-permute-done = f32[64,2000]{1,0:T(8,128)S(1)} collective-permute-done((f32[64,2000]{1,0:T(8,128)S(1)}, f32[64,2000]{1,0:T(8,128)S(1)}, u32[]{:S(2)}, u32[]{:S(2)}) %collective-permute-start) | collective-permute-done | bytes 512032 | tf_op jit(solution)/shard_map/ppermute | solution.py:25
  28.3 0.1 add.28
  28.3 1.9 collective-permute-start.1
  30.2 11.3 %collective-permute-done.1 = f32[64,2000]{1,0:T(8,128)S(1)} collective-permute-done((f32[64,2000]{1,0:T(8,128)S(1)}, f32[64,2000]{1,0:T(8,128)S(1)}, u32[]{:S(2)}, u32[]{:S(2)}) %collective-permute-start.1) | collective-permute-done | bytes 512032 | tf_op jit(solution)/shard_map/ppermute | solution.py:25
  41.5 0.1 add.29
  41.6 2.6 %collective-permute-start.2 = (f32[64,2000]{1,0:T(8,128)S(1)}, f32[64,2000]{1,0:T(8,128)S(1)}, u32[]{:S(2)}, u32[]{:S(2)}) collective-permute-start(f32[64,2000]{1,0:T(8,128)S(1)} %add.29), channel_id=1, source_target_pairs={{0,8},{2,10},{4,12},{6,14},{8,0},{10,2},{12,4},{14,6},{1,9},{3,11}... | collective-permute-start | bytes 1536008 | tf_op jit(solution)/shard_map/ppermute | solution.py:25
  44.2 21.8 %collective-permute-done.2 = f32[64,2000]{1,0:T(8,128)S(1)} collective-permute-done((f32[64,2000]{1,0:T(8,128)S(1)}, f32[64,2000]{1,0:T(8,128)S(1)}, u32[]{:S(2)}, u32[]{:S(2)}) %collective-permute-start.2) | collective-permute-done | bytes 512032 | tf_op jit(solution)/shard_map/ppermute | solution.py:25
  66.0 0.1 add.30
  66.0 1.3 collective-permute-start.3
  67.3 0.0 copy-start.1
  67.4 2.5 %collective-permute-done.3 = f32[64,2000]{1,0:T(8,128)S(1)} collective-permute-done((f32[64,2000]{1,0:T(8,128)S(1)}, f32[64,2000]{1,0:T(8,128)S(1)}, u32[]{:S(2)}, u32[]{:S(2)}) %collective-permute-start.3) | collective-permute-done | bytes 512032 | tf_op jit(solution)/shard_map/ppermute | solution.py:10
  69.8 4.7 %fusion.4 = f32[64,512]{1,0:T(8,128)S(1)} fusion(f32[1,2000,512]{2,1,0:T(8,128)} %param.2, f32[64,2000]{1,0:T(8,128)S(1)} %collective-permute-done.3, f32[64,2000]{1,0:T(8,128)S(1)} %add.30, pred[]{:T(512)S(6)} %eq.4), kind=kOutput, calls=%fused_computation.4 | convolution fusion | flops 786560000 | bytes 5251073 | tf_op jit(solution)/shard_map/dot_general | solution.py:29
  74.6 0.3 fusion.24
  74.9 0.0 copy-done.1
  74.9 4.6 %fusion.2 = f32[64,2000]{1,0:T(8,128)} fusion(f32[64,512]{1,0:T(8,128)S(1)} %fusion.4, f32[1,2000,512]{2,1,0:T(8,128)S(1)} %copy-done.1), kind=kOutput, calls=%fused_computation.2 | convolution fusion | flops 786432000 | bytes 4739072 | tf_op jit(solution)/shard_map/dot_general | solution.py:31
  79.5 37.0 %psum.14 = f32[64,64]{0,1:T(8,128)S(1)} all-reduce(f32[64,64]{0,1:T(8,128)S(1)} %fusion.24), channel_id=1, replica_groups=mesh['groups'=2,'cells'=8,'side'=2] {'cells'}, use_global_device_ids=true, to_apply=%region_0.1 | all-reduce | flops 4096 | bytes 32768 | tf_op jit(solution)/shard_map/psum | solution.py:32
  116.4 0.1 copy.4
  116.5 0.0 all-reduce.2.cloned.1.call-update
  116.6 5.8 %cholesky.16 = f32[64,64]{1,0:T(8,128)S(1)} custom-call(f32[64,64]{1,0:T(8,128)S(1)} %fusion.23), custom_call_target="Cholesky" | custom-call | tf_op jit(solution)/shard_map/jit(cholesky)/cholesky | solution.py:33
  122.4 0.6 compare_reduce_fusion
  123.1 0.7 fusion.19
  123.7 4.9 %custom-call.10 = f32[1,64,64]{1,2,0:T(8,128)S(1)} custom-call(f32[1,64,64]{2,1,0:T(8,128)S(1)} %fusion.19), custom_call_target="InvertDiagBlocksLowerTriangular" | custom-call | tf_op jit(solution)/shard_map/jit(_solve_triangular)/triangular_solve | solution.py:34
  128.6 58.2 %all-reduce.2.cloned.1.call-done = f32[64,2000]{1,0:T(8,128)} async-done(((f32[64,2000]{1,0:T(8,128)}), f32[64,2000]{1,0:T(8,128)}) %all-reduce.2.cloned.1.call-update) | async-done | bytes 512016 | tf_op jit(solution)/shard_map/psum | solution.py:32
  186.8 1.7 fusion.20
  188.5 1.5 collective-permute-start.4
  190.0 0.3 convolution_multiply_fusion
  190.3 1.2 collective-permute-done.4
  191.5 5.4 %fusion.14 = f32[1,64,512]{2,1,0:T(8,128)} fusion(f32[64,512]{1,0:T(8,128)S(1)} %convolution_multiply_fusion, f32[64,2000]{1,0:T(8,128)S(1)} %collective-permute-done.4, f32[1,2000,512]{2,1,0:T(8,128)} %param.2, pred[]{:T(512)S(6)} %eq.4), kind=kOutput, calls=%fused_computation.10 | convolution fusion | flops 786497536 | bytes 4870145 | tf_op jit(solution)/shard_map/dot_general | solution.py:37
  (2 shorter events, 0.0 us)
Async XLA Ops:
  6.5 0.9 copy-start
  6.5 180.3 %all-reduce.2.cloned.1.call-start = ((), (), s32[]{:S(2)}) async-start(), calls=%async_computation | async-start | bytes 1048576 | tf_op jit(solution)/shard_map/psum | solution.py:32
  13.3 15.0 %collective-permute-start = (f32[64,2000]{1,0:T(8,128)S(1)}, f32[64,2000]{1,0:T(8,128)S(1)}, u32[]{:S(2)}, u32[]{:S(2)}) collective-permute-start(f32[64,2000]{1,0:T(8,128)S(1)} %fusion.6), channel_id=1, source_target_pairs={{0,2},{2,0},{4,6},{6,4},{8,10},{10,8},{12,14},{14,12},{1,3},{3,1},... | collective-permute-start | bytes 1536008 | tf_op jit(solution)/shard_map/ppermute | solution.py:25
  28.3 13.1 %collective-permute-start.1 = (f32[64,2000]{1,0:T(8,128)S(1)}, f32[64,2000]{1,0:T(8,128)S(1)}, u32[]{:S(2)}, u32[]{:S(2)}) collective-permute-start(f32[64,2000]{1,0:T(8,128)S(1)} %add.28), channel_id=1, source_target_pairs={{0,4},{2,6},{4,0},{6,2},{8,12},{10,14},{12,8},{14,10},{1,5},{3,7},... | collective-permute-start | bytes 1536008 | tf_op jit(solution)/shard_map/ppermute | solution.py:25
  41.6 24.4 %collective-permute-start.2 = (f32[64,2000]{1,0:T(8,128)S(1)}, f32[64,2000]{1,0:T(8,128)S(1)}, u32[]{:S(2)}, u32[]{:S(2)}) collective-permute-start(f32[64,2000]{1,0:T(8,128)S(1)} %add.29), channel_id=1, source_target_pairs={{0,8},{2,10},{4,12},{6,14},{8,0},{10,2},{12,4},{14,6},{1,9},{3,11}... | collective-permute-start | bytes 1536008 | tf_op jit(solution)/shard_map/ppermute | solution.py:25
  66.0 3.8 %collective-permute-start.3 = (f32[64,2000]{1,0:T(8,128)S(1)}, f32[64,2000]{1,0:T(8,128)S(1)}, u32[]{:S(2)}, u32[]{:S(2)}) collective-permute-start(f32[64,2000]{1,0:T(8,128)S(1)} %add.30), channel_id=1, source_target_pairs={{1,0},{3,2},{5,4},{7,6},{9,8},{11,10},{13,12},{15,14},{17,16},{19,... | collective-permute-start | bytes 1536008 | tf_op jit(solution)/shard_map/ppermute | solution.py:10
  67.3 7.5 %copy-start.1 = (f32[1,2000,512]{2,1,0:T(8,128)S(1)}, f32[1,2000,512]{2,1,0:T(8,128)}, u32[]{:S(2)}) copy-start(f32[1,2000,512]{2,1,0:T(8,128)} %param.2) | copy-start | bytes 12288004
  188.5 3.0 %collective-permute-start.4 = (f32[64,2000]{1,0:T(8,128)S(1)}, f32[64,2000]{1,0:T(8,128)S(1)}, u32[]{:S(2)}, u32[]{:S(2)}) collective-permute-start(f32[64,2000]{1,0:T(8,128)S(1)} %fusion.20), channel_id=1, source_target_pairs={{0,1},{2,3},{4,5},{6,7},{8,9},{10,11},{12,13},{14,15},{16,17},{18,... | collective-permute-start | bytes 1536008 | tf_op jit(solution)/shard_map/ppermute | solution.py:10
Sparse Core Ops, SparseCore 0:
  116.7 70.0 all-reduce.1
